TPU v7x, 768 devices: a whole 4x8x12 slice. The times are simulated.
768 devices in a mesh: gx: 12 (over z), gy: 64 (over y, x, core).
Axes of the slice: x: 4, y: 8, z: 12, core: 2. Of those that a mesh axis runs over, the one named last changes fastest.
Arguments:
- rock_class: int32 [96, 1024, 128], P('gx', 'gy'), may hold values from 0 to 15
- well_mask: int32 [96, 1024, 128], P('gx', 'gy'), may hold values 0 or 1
- perm_table: float32 [16], replicated, may hold values from 0.01 to 1
- poro_table: float32 [16], replicated, may hold values from 0.05 to 0.35
- accum: float32 [3, 3, 96, 1024, 128], P(None, None, 'gx', 'gy'), may hold values from -0.6 to 2, as said below
- mobility: float32 [3, 96, 1024, 128], P(None, 'gx', 'gy'), may hold values from 0.2 to 2
- right_side: float32 [3, 96, 1024, 128], P(None, 'gx', 'gy'), may hold values from -30 to 30
Outputs:
- pressure: float32 [96, 1024, 128], P('gx', 'gy')
- correction: float32 [3, 96, 1024, 128], P(None, 'gx', 'gy')
Inputs may be any that keep to these rules, and one draw needn't show every extreme that they name: `accum`: in each cell's 3 x 3 block the diagonal entries are positive and every off-diagonal entry is at most 0.3 times its row's diagonal entry in magnitude.
All inputs are finite; a program needn't handle non-finite values. No bound on the sum of `well_mask` on one device may be relied on, other than what follows from the above.
Results may differ from a plain program's by a relative error of at most 0.0001.
Values sent between devices are 32-bit elements; how exact they have to be, the bound alone decides.
A program may use at most 32 MiB of HBM per device.

v0:
```python
import functools

import jax
import jax.numpy as jnp
from jax import lax
from jax.sharding import Mesh
from jax.sharding import PartitionSpec as P

ITERS = 3
GX_GY = ("gx", "gy_0", "gy_1", "gy_2")
GY = ("gy_0", "gy_1", "gy_2")


FACE_X = 1.0
FACE_Y = 1.0
FACE_Z = 2.0
WELL_FACTOR = 4.0


def padded_2(value, sides, width):
    for axis, dim in sides:
        devices, length = (lax.axis_size(axis), value.shape[dim])
        up = [(i, (i + 1) % devices) for i in range(devices - 1)]
        down = [(j, i) for i, j in up]
        last = lax.slice_in_dim(value, length - width, length, axis=dim)
        initial = lax.slice_in_dim(value, 0, width, axis=dim)
        before = lax.ppermute(last, axis, up)
        after = lax.ppermute(initial, axis, down)
        value = jnp.concatenate([before, value, after], axis=dim)
    return value


def padded_3(value, sides, width):
    edges = {}
    for axis, dim in sides:
        devices, length = (lax.axis_size(axis), value.shape[dim])
        up = [(i, (i + 1) % devices) for i in range(devices - 1)]
        last = lax.slice_in_dim(value, length - width, length, axis=dim)
        initial = lax.slice_in_dim(value, 0, width, axis=dim)
        edges[dim] = (
            lax.ppermute(last, axis, up),
            lax.ppermute(initial, axis, [(b, a) for a, b in up]),
        )
    done = []
    for _, dim in sides:
        low, high = edges[dim]
        around = [(width, width) if d in done else (0, 0) for d in range(value.ndim)]
        value = jnp.concatenate([jnp.pad(low, around), value, jnp.pad(high, around)], axis=dim)
        done.append(dim)
    return value


def over_axes(value, axes):
    return functools.reduce(lax.psum, axes, value)


def harmonic(left_perm, right_perm, left_safe, right_safe):
    return 2.0 * left_perm * right_perm / (left_safe + right_safe)


def couplings(perm_ext, safe_ext, mobility_ext):
    row_perm = perm_ext[:, 1:-1]
    row_safe = safe_ext[:, 1:-1]
    row_mobility = mobility_ext[:, :, 1:-1]
    cross_x = (
        FACE_X
        * harmonic(row_perm[:-1], row_perm[1:], row_safe[:-1], row_safe[1:])
        * 0.5
        * (row_mobility[:, :-1] + row_mobility[:, 1:])
    )
    column_perm = perm_ext[1:-1]
    column_safe = safe_ext[1:-1]
    column_mobility = mobility_ext[:, 1:-1]
    cross_y = (
        FACE_Y
        * harmonic(column_perm[:, :-1], column_perm[:, 1:], column_safe[:, :-1], column_safe[:, 1:])
        * 0.5
        * (column_mobility[:, :, :-1] + column_mobility[:, :, 1:])
    )
    center_perm = perm_ext[1:-1, 1:-1]
    center_safe = safe_ext[1:-1, 1:-1]
    center_mobility = mobility_ext[:, 1:-1, 1:-1]
    vertical = (
        FACE_Z
        * harmonic(
            center_perm[:, :, :-1],
            center_perm[:, :, 1:],
            center_safe[:, :, :-1],
            center_safe[:, :, 1:],
        )
        * 0.5
        * (center_mobility[..., :-1] + center_mobility[..., 1:])
    )
    closed = jnp.zeros(vertical.shape[:-1] + (1,), jnp.float32)
    cross_z = jnp.concatenate([closed, vertical, closed], axis=-1)
    return (cross_x, cross_y, cross_z)


def face_flux(coupling, field_ext):
    cross_x, cross_y, cross_z = coupling
    center = field_ext[..., 1:-1, 1:-1, :]
    closed = jnp.zeros_like(center[..., :1])
    lifted = jnp.concatenate([closed, center, closed], axis=-1)
    totals = cross_x[..., 1:, :, :] * (center - field_ext[..., 2:, 1:-1, :])
    totals = totals + cross_x[..., :-1, :, :] * (center - field_ext[..., :-2, 1:-1, :])
    totals = totals + cross_y[..., :, 1:, :] * (center - field_ext[..., 1:-1, 2:, :])
    totals = totals + cross_y[..., :, :-1, :] * (center - field_ext[..., 1:-1, :-2, :])
    totals = totals + cross_z[..., 1:] * (center - lifted[..., 2:])
    totals = totals + cross_z[..., :-1] * (center - lifted[..., :-2])
    return totals


def phase_diagonal(coupling):
    cross_x, cross_y, cross_z = coupling
    totals = cross_x[..., 1:, :, :] + cross_x[..., :-1, :, :]
    totals = totals + cross_y[..., :, 1:, :] + cross_y[..., :, :-1, :]
    return totals + cross_z[..., 1:] + cross_z[..., :-1]


def identity_blocks():
    return jnp.eye(3, dtype=jnp.float32)[:, :, None, None, None]


def invert_blocks(blocks):

    def cofactor(row_index, column_index):
        next_row = (row_index + 1) % 3
        last_row = (row_index + 2) % 3
        next_col = (column_index + 1) % 3
        last_col = (column_index + 2) % 3
        return (
            blocks[next_row, next_col] * blocks[last_row, last_col]
            - blocks[next_row, last_col] * blocks[last_row, next_col]
        )

    adjugate = jnp.stack(
        [
            jnp.stack([cofactor(column_index, row_index) for column_index in range(3)])
            for row_index in range(3)
        ]
    )
    determinant = jnp.sum(blocks[0] * adjugate[:, 0], axis=0)
    return adjugate / determinant


def jacobian(storage_block, coupling, phase_well, center, field_ext):
    return (
        jnp.sum(storage_block * center[None], axis=1)
        + face_flux(coupling, field_ext)
        + phase_well * center
    )


def shards(rock_class, well_mask, perm_table, poro_table, accum, mobility, right_side):
    classes = perm_table.shape[0]
    onehot = (rock_class[None] == jnp.arange(classes, dtype=jnp.int32)[:, None, None, None]).astype(
        jnp.float32
    )
    looked = jnp.einsum(
        "tk,kxyz->txyz",
        jnp.stack([perm_table, poro_table]),
        onehot,
        precision=lax.Precision.HIGHEST,
    )
    permeability = looked[0]
    porosity = looked[1]
    storage_block = porosity * accum
    well_term = WELL_FACTOR * permeability * well_mask.astype(jnp.float32)
    phase_well = well_term * mobility
    stacked = jnp.concatenate([permeability[None], mobility], axis=0)
    rimmed = padded_2(stacked, (("gx", 1), (GY, 2)), 1)
    coupling = couplings(rimmed[0], rimmed[0], rimmed[1:4])
    inverse = invert_blocks(
        storage_block + identity_blocks() * (phase_diagonal(coupling) + phase_well)
    )
    summed = tuple((jnp.sum(member, axis=0) for member in coupling))
    storage = jnp.sum(storage_block, axis=(0, 1)) + well_term * jnp.sum(mobility, axis=0)

    def pressure_operator(pressure_field):
        padded = padded_3(pressure_field, (("gx", 0), (GY, 1)), 1)
        return storage * pressure_field + face_flux(summed, padded)

    source = jnp.sum(right_side, axis=0)
    solution = jnp.zeros_like(source)
    residual = source
    applied = pressure_operator(residual)
    direction = jnp.zeros_like(source)
    carried = jnp.zeros_like(source)
    bent = jnp.zeros_like(source)
    norm_old = None
    step_old = None
    for iteration in range(ITERS):
        norm_now, curvature = (
            over_axes(jnp.sum(residual * residual), GX_GY),
            over_axes(jnp.sum(applied * residual), GX_GY),
        )
        if iteration + 1 < ITERS:
            images = pressure_operator(applied)
        if iteration == 0:
            mixing = 0.0
            step_size = norm_now / curvature
        else:
            mixing = norm_now / norm_old
            step_size = norm_now / (curvature - mixing * norm_now / step_old)
        if iteration + 1 < ITERS:
            bent = images + mixing * bent
        carried = applied + mixing * carried
        direction = residual + mixing * direction
        solution = solution + step_size * direction
        residual = residual - step_size * carried
        if iteration + 1 < ITERS:
            applied = applied - step_size * bent
        norm_old = norm_now
        step_old = step_size
    pressure_cycle = padded_3(solution, (("gx", 0), (GY, 1)), 1)
    start_ext = jnp.broadcast_to(pressure_cycle[None], (3,) + pressure_cycle.shape)
    start_center = start_ext[:, 1:-1, 1:-1]
    defect = right_side - jacobian(storage_block, coupling, phase_well, start_center, start_ext)
    update = start_center + jnp.sum(inverse * defect[None], axis=1)
    update_cycle = padded_3(update, (("gx", 1), (GY, 2)), 1)
    defect = right_side - jacobian(storage_block, coupling, phase_well, update, update_cycle)
    correction = update + jnp.sum(inverse * defect[None], axis=1)
    return (solution, correction)


def solution(mesh):
    finer = Mesh(mesh.devices.reshape(mesh.shape["gx"], 8, 4, 2), ("gx", "gy_0", "gy_1", "gy_2"))
    in_specs = (
        P("gx", GY, None),
        P("gx", GY, None),
        P(),
        P(),
        P(None, None, "gx", GY, None),
        P(None, "gx", GY, None),
        P(None, "gx", GY, None),
    )
    out_specs = (P("gx", GY, None), P(None, "gx", GY, None))
    return jax.shard_map(
        shards, mesh=finer, in_specs=in_specs, out_specs=out_specs, check_vma=False
    )
```

profile of v0, /device:TPU:1, one launch (start us, length us, event | category | flops | bytes accessed | tf_op | source)
XLA Modules:
  0.0 264.2 jit_solution(17226770452885656585)
XLA Ops:
  1.6 12.4 %collective-permute-start.6 = (f32[8,1,128]{2,1,0:T(1,128)S(1)}, f32[8,1,128]{2,1,0:T(1,128)S(1)}, u32[]{:S(2)}, u32[]{:S(2)}) collective-permute-start(f32[8,1,128]{2,1,0:T(1,128)S(1)} %get-tuple-element.76), channel_id=1, source_target_pairs={{1,0},{2,1},{3,2},{4,3},{5,4},{6,5},{7,6},{8,7},{9,8},{10,9},{11,1... | collective-permute-start | bytes 12296 | tf_op jit(solution)/shard_map/ppermute | solution.py:42
  20.6 4.0 %collective-permute-start.5 = (f32[1,16,128]{2,1,0:T(8,128)S(1)}, f32[1,16,128]{2,1,0:T(8,128)S(1)}, u32[]{:S(2)}, u32[]{:S(2)}) collective-permute-start(f32[1,16,128]{2,1,0:T(8,128)S(1)} %get-tuple-element.78), channel_id=1, source_target_pairs={{0,64},{64,128},{128,192},{192,256},{256,320},{320,384},{384,448},... | collective-permute-start | bytes 24584 | tf_op jit(solution)/shard_map/ppermute | solution.py:41
  26.6 2.4 collective-permute-start.3
  36.7 3.8 %collective-permute-start.11 = (f32[8,1,128]{2,1,0:T(1,128)S(1)}, f32[8,1,128]{2,1,0:T(1,128)S(1)}, u32[]{:S(2)}, u32[]{:S(2)}) collective-permute-start(f32[8,1,128]{2,1,0:T(1,128)S(1)} %get-tuple-element.73), channel_id=1, source_target_pairs={{0,1},{1,2},{2,3},{3,4},{4,5},{5,6},{6,7},{7,8},{8,9},{9,10},{10,1... | collective-permute-start | bytes 12296 | tf_op jit(solution)/shard_map/ppermute | solution.py:41
  44.0 25.3 %all-reduce.24 = (f32[]{:T(128)}, f32[]{:T(128)}) all-reduce(f32[]{:T(128)} %get-tuple-element.5, f32[]{:T(128)} %get-tuple-element.4), channel_id=1, replica_groups=mesh['gx'=12,'gy_0'=8,'gy_1'=4,'gy_2'=2] {'gx'}, use_global_device_ids=true, to_apply=%region_2.0 | all-reduce | flops 2 | bytes 16 | tf_op jit(solution)/shard_map/psum | solution.py:54
  69.2 18.1 %all-reduce.27 = (f32[]{:T(128)}, f32[]{:T(128)}) all-reduce(f32[]{:T(128)} %get-tuple-element.10, f32[]{:T(128)} %get-tuple-element.11), channel_id=1, replica_groups=mesh['gx'=12,'gy_0'=8,'gy_1'=4,'gy_2'=2] {'gy_0'}, use_global_device_ids=true, to_apply=%region_3.0 | all-reduce | flops 2 | bytes 16 | tf_op jit(solution)/shard_map/psum | solution.py:54
  87.3 11.0 %all-reduce.30 = (f32[]{:T(128)}, f32[]{:T(128)}) all-reduce(f32[]{:T(128)} %get-tuple-element.16, f32[]{:T(128)} %get-tuple-element.17), channel_id=1, replica_groups=mesh['gx'=12,'gy_0'=8,'gy_1'=4,'gy_2'=2] {'gy_1'}, use_global_device_ids=true, to_apply=%region_4.0 | all-reduce | flops 2 | bytes 16 | tf_op jit(solution)/shard_map/psum | solution.py:54
  98.3 10.0 %all-reduce.33 = (f32[]{:T(128)}, f32[]{:T(128)}) all-reduce(f32[]{:T(128)} %get-tuple-element.22, f32[]{:T(128)} %get-tuple-element.23), channel_id=1, replica_groups=mesh['gx'=12,'gy_0'=8,'gy_1'=4,'gy_2'=2] {'gy_2'}, use_global_device_ids=true, to_apply=%region_5.0 | all-reduce | flops 2 | bytes 16 | tf_op jit(solution)/shard_map/psum | solution.py:54
  110.5 17.0 %all-reduce.23 = (f32[]{:T(128)}, f32[]{:T(128)}) all-reduce(f32[]{:T(128)} %get-tuple-element.3, f32[]{:T(128)} %get-tuple-element.2), channel_id=1, replica_groups=mesh['gx'=12,'gy_0'=8,'gy_1'=4,'gy_2'=2] {'gx'}, use_global_device_ids=true, to_apply=%region_17.18 | all-reduce | flops 2 | bytes 16 | tf_op jit(solution)/shard_map/psum | solution.py:54
  127.5 13.1 %all-reduce.26 = (f32[]{:T(128)}, f32[]{:T(128)}) all-reduce(f32[]{:T(128)} %get-tuple-element.8, f32[]{:T(128)} %get-tuple-element.9), channel_id=1, replica_groups=mesh['gx'=12,'gy_0'=8,'gy_1'=4,'gy_2'=2] {'gy_0'}, use_global_device_ids=true, to_apply=%region_18.19 | all-reduce | flops 2 | bytes 16 | tf_op jit(solution)/shard_map/psum | solution.py:54
  140.6 8.4 %all-reduce.29 = (f32[]{:T(128)}, f32[]{:T(128)}) all-reduce(f32[]{:T(128)} %get-tuple-element.14, f32[]{:T(128)} %get-tuple-element.15), channel_id=1, replica_groups=mesh['gx'=12,'gy_0'=8,'gy_1'=4,'gy_2'=2] {'gy_1'}, use_global_device_ids=true, to_apply=%region_19.20 | all-reduce | flops 2 | bytes 16 | tf_op jit(solution)/shard_map/psum | solution.py:54
  149.0 14.3 %all-reduce.32 = (f32[]{:T(128)}, f32[]{:T(128)}) all-reduce(f32[]{:T(128)} %get-tuple-element.20, f32[]{:T(128)} %get-tuple-element.21), channel_id=1, replica_groups=mesh['gx'=12,'gy_0'=8,'gy_1'=4,'gy_2'=2] {'gy_2'}, use_global_device_ids=true, to_apply=%region_20.21 | all-reduce | flops 2 | bytes 16 | tf_op jit(solution)/shard_map/psum | solution.py:54
  170.1 3.3 %collective-permute-start.15 = (f32[8,1,128]{2,1,0:T(1,128)S(1)}, f32[8,1,128]{2,1,0:T(1,128)S(1)}, u32[]{:S(2)}, u32[]{:S(2)}) collective-permute-start(f32[8,1,128]{2,1,0:T(1,128)S(1)} %get-tuple-element.69), channel_id=1, source_target_pairs={{0,1},{1,2},{2,3},{3,4},{4,5},{5,6},{6,7},{7,8},{8,9},{9,10},{10,1... | collective-permute-start | bytes 12296 | tf_op jit(solution)/shard_map/ppermute | solution.py:41
  173.4 2.5 collective-permute-start.13
  177.9 2.6 collective-permute-done.12
  181.4 18.4 %all-reduce.22 = (f32[]{:T(128)}, f32[]{:T(128)}) all-reduce(f32[]{:T(128)} %multiply_reduce_fusion.5, f32[]{:T(128)} %fusion.110), channel_id=1, replica_groups=mesh['gx'=12,'gy_0'=8,'gy_1'=4,'gy_2'=2] {'gx'}, use_global_device_ids=true, to_apply=%region_27.28 | all-reduce | flops 2 | bytes 16 | tf_op jit(solution)/shard_map/psum | solution.py:54
  199.7 11.3 %all-reduce.25 = (f32[]{:T(128)}, f32[]{:T(128)}) all-reduce(f32[]{:T(128)} %get-tuple-element.6, f32[]{:T(128)} %get-tuple-element.7), channel_id=1, replica_groups=mesh['gx'=12,'gy_0'=8,'gy_1'=4,'gy_2'=2] {'gy_0'}, use_global_device_ids=true, to_apply=%region_28.29 | all-reduce | flops 2 | bytes 16 | tf_op jit(solution)/shard_map/psum | solution.py:54
  211.1 8.8 %all-reduce.28 = (f32[]{:T(128)}, f32[]{:T(128)}) all-reduce(f32[]{:T(128)} %get-tuple-element.12, f32[]{:T(128)} %get-tuple-element.13), channel_id=1, replica_groups=mesh['gx'=12,'gy_0'=8,'gy_1'=4,'gy_2'=2] {'gy_1'}, use_global_device_ids=true, to_apply=%region_29.30 | all-reduce | flops 2 | bytes 16 | tf_op jit(solution)/shard_map/psum | solution.py:54
  219.9 12.8 %all-reduce.31 = (f32[]{:T(128)}, f32[]{:T(128)}) all-reduce(f32[]{:T(128)} %get-tuple-element.18, f32[]{:T(128)} %get-tuple-element.19), channel_id=1, replica_groups=mesh['gx'=12,'gy_0'=8,'gy_1'=4,'gy_2'=2] {'gy_2'}, use_global_device_ids=true, to_apply=%region_30.31 | all-reduce | flops 2 | bytes 16 | tf_op jit(solution)/shard_map/psum | solution.py:54
  239.2 3.3 %collective-permute-start.19 = (f32[8,1,128]{2,1,0:T(1,128)S(1)}, f32[8,1,128]{2,1,0:T(1,128)S(1)}, u32[]{:S(2)}, u32[]{:S(2)}) collective-permute-start(f32[8,1,128]{2,1,0:T(1,128)S(1)} %get-tuple-element.65), channel_id=1, source_target_pairs={{0,1},{1,2},{2,3},{3,4},{4,5},{5,6},{6,7},{7,8},{8,9},{9,10},{10,1... | collective-permute-start | bytes 12296 | tf_op jit(solution)/shard_map/ppermute | solution.py:41
  245.3 3.0 %collective-permute-done.16 = f32[1,16,128]{2,1,0:T(8,128)S(1)} collective-permute-done((f32[1,16,128]{2,1,0:T(8,128)S(1)}, f32[1,16,128]{2,1,0:T(8,128)S(1)}, u32[]{:S(2)}, u32[]{:S(2)}) %collective-permute-start.16) | collective-permute-done | bytes 8224 | tf_op jit(solution)/shard_map/ppermute | solution.py:42
  252.1 3.3 %collective-permute-start.23 = (f32[3,8,1,128]{3,2,1,0:T(1,128)S(1)}, f32[3,8,1,128]{3,2,1,0:T(1,128)S(1)}, u32[]{:S(2)}, u32[]{:S(2)}) collective-permute-start(f32[3,8,1,128]{3,2,1,0:T(1,128)S(1)} %get-tuple-element.54), channel_id=1, source_target_pairs={{0,1},{1,2},{2,3},{3,4},{4,5},{5,6},{6,7},{7,8},{8,9},{9,10},{10,1... | collective-permute-start | bytes 36872 | tf_op jit(solution)/shard_map/ppermute | solution.py:41
  255.3 2.8 %collective-permute-start.21 = (f32[3,1,16,128]{3,2,1,0:T(8,128)S(1)}, f32[3,1,16,128]{3,2,1,0:T(8,128)S(1)}, u32[]{:S(2)}, u32[]{:S(2)}) collective-permute-start(f32[3,1,16,128]{3,2,1,0:T(8,128)S(1)} %get-tuple-element.55), channel_id=1, source_target_pairs={{0,64},{64,128},{128,192},{192,256},{256,320},{320,384},{384,448},... | collective-permute-start | bytes 73736 | tf_op jit(solution)/shard_map/ppermute | solution.py:41
  259.6 3.6 %collective-permute-done.20 = f32[3,1,16,128]{3,2,1,0:T(8,128)S(1)} collective-permute-done((f32[3,1,16,128]{3,2,1,0:T(8,128)S(1)}, f32[3,1,16,128]{3,2,1,0:T(8,128)S(1)}, u32[]{:S(2)}, u32[]{:S(2)}) %collective-permute-start.20) | collective-permute-done | bytes 24608 | tf_op jit(solution)/shard_map/ppermute | solution.py:42
  (104 shorter events, 37.7 us)
Async XLA Ops:
  1.6 30.7 %collective-permute-start.6 = (f32[8,1,128]{2,1,0:T(1,128)S(1)}, f32[8,1,128]{2,1,0:T(1,128)S(1)}, u32[]{:S(2)}, u32[]{:S(2)}) collective-permute-start(f32[8,1,128]{2,1,0:T(1,128)S(1)} %get-tuple-element.76), channel_id=1, source_target_pairs={{1,0},{2,1},{3,2},{4,3},{5,4},{6,5},{7,6},{8,7},{9,8},{10,9},{11,1... | collective-permute-start | bytes 12296 | tf_op jit(solution)/shard_map/ppermute | solution.py:42
  14.0 18.3 %collective-permute-start.7 = (f32[8,1,128]{2,1,0:T(1,128)S(1)}, f32[8,1,128]{2,1,0:T(1,128)S(1)}, u32[]{:S(2)}, u32[]{:S(2)}) collective-permute-start(f32[8,1,128]{2,1,0:T(1,128)S(1)} %get-tuple-element.77), channel_id=1, source_target_pairs={{0,1},{1,2},{2,3},{3,4},{4,5},{5,6},{6,7},{7,8},{8,9},{9,10},{10,1... | collective-permute-start | bytes 12296 | tf_op jit(solution)/shard_map/ppermute | solution.py:41
  18.0 6.6 %collective-permute-start = (f32[4,1,16,128]{3,2,1,0:T(8,128)S(1)}, f32[4,1,16,128]{3,2,1,0:T(8,128)S(1)}, u32[]{:S(2)}, u32[]{:S(2)}) collective-permute-start(f32[4,1,16,128]{3,2,1,0:T(8,128)S(1)} %get-tuple-element.51), channel_id=1, source_target_pairs={{0,64},{64,128},{128,192},{192,256},{256,320},{320,384},{384,448},... | collective-permute-start | bytes 98312 | tf_op jit(solution)/shard_map/ppermute | solution.py:27
  19.3 5.3 %collective-permute-start.1 = (f32[4,1,16,128]{3,2,1,0:T(8,128)S(1)}, f32[4,1,16,128]{3,2,1,0:T(8,128)S(1)}, u32[]{:S(2)}, u32[]{:S(2)}) collective-permute-start(f32[4,1,16,128]{3,2,1,0:T(8,128)S(1)} %get-tuple-element.52), channel_id=1, source_target_pairs={{64,0},{128,64},{192,128},{256,192},{320,256},{384,320},{448,384},... | collective-permute-start | bytes 98312 | tf_op jit(solution)/shard_map/ppermute | solution.py:28
  20.6 11.8 %collective-permute-start.5 = (f32[1,16,128]{2,1,0:T(8,128)S(1)}, f32[1,16,128]{2,1,0:T(8,128)S(1)}, u32[]{:S(2)}, u32[]{:S(2)}) collective-permute-start(f32[1,16,128]{2,1,0:T(8,128)S(1)} %get-tuple-element.78), channel_id=1, source_target_pairs={{0,64},{64,128},{128,192},{192,256},{256,320},{320,384},{384,448},... | collective-permute-start | bytes 24584 | tf_op jit(solution)/shard_map/ppermute | solution.py:41
  24.6 4.4 %collective-permute-start.2 = (f32[4,10,1,128]{3,2,1,0:T(1,128)S(1)}, f32[4,10,1,128]{3,2,1,0:T(1,128)S(1)}, u32[]{:S(2)}, u32[]{:S(2)}) collective-permute-start(f32[4,10,1,128]{3,2,1,0:T(1,128)S(1)} %get-tuple-element.49), channel_id=1, source_target_pairs={{0,1},{1,2},{2,3},{3,4},{4,5},{5,6},{6,7},{7,8},{8,9},{9,10},{10,1... | collective-permute-start | bytes 61448 | tf_op jit(solution)/shard_map/ppermute | solution.py:27
  26.6 5.1 %collective-permute-start.3 = (f32[4,10,1,128]{3,2,1,0:T(1,128)S(1)}, f32[4,10,1,128]{3,2,1,0:T(1,128)S(1)}, u32[]{:S(2)}, u32[]{:S(2)}) collective-permute-start(f32[4,10,1,128]{3,2,1,0:T(1,128)S(1)} %get-tuple-element.50), channel_id=1, source_target_pairs={{1,0},{2,1},{3,2},{4,3},{5,4},{6,5},{7,6},{8,7},{9,8},{10,9},{11,1... | collective-permute-start | bytes 61448 | tf_op jit(solution)/shard_map/ppermute | solution.py:28
  29.1 4.5 %collective-permute-start.4 = (f32[1,16,128]{2,1,0:T(8,128)S(1)}, f32[1,16,128]{2,1,0:T(8,128)S(1)}, u32[]{:S(2)}, u32[]{:S(2)}) collective-permute-start(f32[1,16,128]{2,1,0:T(8,128)S(1)} %get-tuple-element.79), channel_id=1, source_target_pairs={{64,0},{128,64},{192,128},{256,192},{320,256},{384,320},{448,384},... | collective-permute-start | bytes 24584 | tf_op jit(solution)/shard_map/ppermute | solution.py:42
  34.4 75.2 %collective-permute-start.10 = (f32[8,1,128]{2,1,0:T(1,128)S(1)}, f32[8,1,128]{2,1,0:T(1,128)S(1)}, u32[]{:S(2)}, u32[]{:S(2)}) collective-permute-start(f32[8,1,128]{2,1,0:T(1,128)S(1)} %get-tuple-element.72), channel_id=1, source_target_pairs={{1,0},{2,1},{3,2},{4,3},{5,4},{6,5},{7,6},{8,7},{9,8},{10,9},{11,1... | collective-permute-start | bytes 12296 | tf_op jit(solution)/shard_map/ppermute | solution.py:42
  36.7 72.9 %collective-permute-start.11 = (f32[8,1,128]{2,1,0:T(1,128)S(1)}, f32[8,1,128]{2,1,0:T(1,128)S(1)}, u32[]{:S(2)}, u32[]{:S(2)}) collective-permute-start(f32[8,1,128]{2,1,0:T(1,128)S(1)} %get-tuple-element.73), channel_id=1, source_target_pairs={{0,1},{1,2},{2,3},{3,4},{4,5},{5,6},{6,7},{7,8},{8,9},{9,10},{10,1... | collective-permute-start | bytes 12296 | tf_op jit(solution)/shard_map/ppermute | solution.py:41
  40.5 69.1 %collective-permute-start.9 = (f32[1,16,128]{2,1,0:T(8,128)S(1)}, f32[1,16,128]{2,1,0:T(8,128)S(1)}, u32[]{:S(2)}, u32[]{:S(2)}) collective-permute-start(f32[1,16,128]{2,1,0:T(8,128)S(1)} %get-tuple-element.74), channel_id=1, source_target_pairs={{0,64},{64,128},{128,192},{192,256},{256,320},{320,384},{384,448},... | collective-permute-start | bytes 24584 | tf_op jit(solution)/shard_map/ppermute | solution.py:41
  42.7 66.9 %collective-permute-start.8 = (f32[1,16,128]{2,1,0:T(8,128)S(1)}, f32[1,16,128]{2,1,0:T(8,128)S(1)}, u32[]{:S(2)}, u32[]{:S(2)}) collective-permute-start(f32[1,16,128]{2,1,0:T(8,128)S(1)} %get-tuple-element.75), channel_id=1, source_target_pairs={{64,0},{128,64},{192,128},{256,192},{320,256},{384,320},{448,384},... | collective-permute-start | bytes 24584 | tf_op jit(solution)/shard_map/ppermute | solution.py:42
  167.8 10.1 %collective-permute-start.14 = (f32[8,1,128]{2,1,0:T(1,128)S(1)}, f32[8,1,128]{2,1,0:T(1,128)S(1)}, u32[]{:S(2)}, u32[]{:S(2)}) collective-permute-start(f32[8,1,128]{2,1,0:T(1,128)S(1)} %get-tuple-element.68), channel_id=1, source_target_pairs={{1,0},{2,1},{3,2},{4,3},{5,4},{6,5},{7,6},{8,7},{9,8},{10,9},{11,1... | collective-permute-start | bytes 12296 | tf_op jit(solution)/shard_map/ppermute | solution.py:42
  170.1 7.8 %collective-permute-start.15 = (f32[8,1,128]{2,1,0:T(1,128)S(1)}, f32[8,1,128]{2,1,0:T(1,128)S(1)}, u32[]{:S(2)}, u32[]{:S(2)}) collective-permute-start(f32[8,1,128]{2,1,0:T(1,128)S(1)} %get-tuple-element.69), channel_id=1, source_target_pairs={{0,1},{1,2},{2,3},{3,4},{4,5},{5,6},{6,7},{7,8},{8,9},{9,10},{10,1... | collective-permute-start | bytes 12296 | tf_op jit(solution)/shard_map/ppermute | solution.py:41
  173.4 4.5 %collective-permute-start.13 = (f32[1,16,128]{2,1,0:T(8,128)S(1)}, f32[1,16,128]{2,1,0:T(8,128)S(1)}, u32[]{:S(2)}, u32[]{:S(2)}) collective-permute-start(f32[1,16,128]{2,1,0:T(8,128)S(1)} %get-tuple-element.70), channel_id=1, source_target_pairs={{0,64},{64,128},{128,192},{192,256},{256,320},{320,384},{384,448},... | collective-permute-start | bytes 24584 | tf_op jit(solution)/shard_map/ppermute | solution.py:41
  176.0 4.5 %collective-permute-start.12 = (f32[1,16,128]{2,1,0:T(8,128)S(1)}, f32[1,16,128]{2,1,0:T(8,128)S(1)}, u32[]{:S(2)}, u32[]{:S(2)}) collective-permute-start(f32[1,16,128]{2,1,0:T(8,128)S(1)} %get-tuple-element.71), channel_id=1, source_target_pairs={{64,0},{128,64},{192,128},{256,192},{320,256},{384,320},{448,384},... | collective-permute-start | bytes 24584 | tf_op jit(solution)/shard_map/ppermute | solution.py:42
  237.0 8.3 %collective-permute-start.18 = (f32[8,1,128]{2,1,0:T(1,128)S(1)}, f32[8,1,128]{2,1,0:T(1,128)S(1)}, u32[]{:S(2)}, u32[]{:S(2)}) collective-permute-start(f32[8,1,128]{2,1,0:T(1,128)S(1)} %get-tuple-element.64), channel_id=1, source_target_pairs={{1,0},{2,1},{3,2},{4,3},{5,4},{6,5},{7,6},{8,7},{9,8},{10,9},{11,1... | collective-permute-start | bytes 12296 | tf_op jit(solution)/shard_map/ppermute | solution.py:42
  239.2 6.0 %collective-permute-start.19 = (f32[8,1,128]{2,1,0:T(1,128)S(1)}, f32[8,1,128]{2,1,0:T(1,128)S(1)}, u32[]{:S(2)}, u32[]{:S(2)}) collective-permute-start(f32[8,1,128]{2,1,0:T(1,128)S(1)} %get-tuple-element.65), channel_id=1, source_target_pairs={{0,1},{1,2},{2,3},{3,4},{4,5},{5,6},{6,7},{7,8},{8,9},{9,10},{10,1... | collective-permute-start | bytes 12296 | tf_op jit(solution)/shard_map/ppermute | solution.py:41
  242.6 2.7 %collective-permute-start.17 = (f32[1,16,128]{2,1,0:T(8,128)S(1)}, f32[1,16,128]{2,1,0:T(8,128)S(1)}, u32[]{:S(2)}, u32[]{:S(2)}) collective-permute-start(f32[1,16,128]{2,1,0:T(8,128)S(1)} %get-tuple-element.66), channel_id=1, source_target_pairs={{0,64},{64,128},{128,192},{192,256},{256,320},{320,384},{384,448},... | collective-permute-start | bytes 24584 | tf_op jit(solution)/shard_map/ppermute | solution.py:41
  243.9 4.5 %collective-permute-start.16 = (f32[1,16,128]{2,1,0:T(8,128)S(1)}, f32[1,16,128]{2,1,0:T(8,128)S(1)}, u32[]{:S(2)}, u32[]{:S(2)}) collective-permute-start(f32[1,16,128]{2,1,0:T(8,128)S(1)} %get-tuple-element.67), channel_id=1, source_target_pairs={{64,0},{128,64},{192,128},{256,192},{320,256},{384,320},{448,384},... | collective-permute-start | bytes 24584 | tf_op jit(solution)/shard_map/ppermute | solution.py:42
  249.8 9.8 %collective-permute-start.22 = (f32[3,8,1,128]{3,2,1,0:T(1,128)S(1)}, f32[3,8,1,128]{3,2,1,0:T(1,128)S(1)}, u32[]{:S(2)}, u32[]{:S(2)}) collective-permute-start(f32[3,8,1,128]{3,2,1,0:T(1,128)S(1)} %get-tuple-element.53), channel_id=1, source_target_pairs={{1,0},{2,1},{3,2},{4,3},{5,4},{6,5},{7,6},{8,7},{9,8},{10,9},{11,1... | collective-permute-start | bytes 36872 | tf_op jit(solution)/shard_map/ppermute | solution.py:42
  252.1 7.5 %collective-permute-start.23 = (f32[3,8,1,128]{3,2,1,0:T(1,128)S(1)}, f32[3,8,1,128]{3,2,1,0:T(1,128)S(1)}, u32[]{:S(2)}, u32[]{:S(2)}) collective-permute-start(f32[3,8,1,128]{3,2,1,0:T(1,128)S(1)} %get-tuple-element.54), channel_id=1, source_target_pairs={{0,1},{1,2},{2,3},{3,4},{4,5},{5,6},{6,7},{7,8},{8,9},{9,10},{10,1... | collective-permute-start | bytes 36872 | tf_op jit(solution)/shard_map/ppermute | solution.py:41
  255.3 4.2 %collective-permute-start.21 = (f32[3,1,16,128]{3,2,1,0:T(8,128)S(1)}, f32[3,1,16,128]{3,2,1,0:T(8,128)S(1)}, u32[]{:S(2)}, u32[]{:S(2)}) collective-permute-start(f32[3,1,16,128]{3,2,1,0:T(8,128)S(1)} %get-tuple-element.55), channel_id=1, source_target_pairs={{0,64},{64,128},{128,192},{192,256},{256,320},{320,384},{384,448},... | collective-permute-start | bytes 73736 | tf_op jit(solution)/shard_map/ppermute | solution.py:41
  258.2 5.0 %collective-permute-start.20 = (f32[3,1,16,128]{3,2,1,0:T(8,128)S(1)}, f32[3,1,16,128]{3,2,1,0:T(8,128)S(1)}, u32[]{:S(2)}, u32[]{:S(2)}) collective-permute-start(f32[3,1,16,128]{3,2,1,0:T(8,128)S(1)} %get-tuple-element.56), channel_id=1, source_target_pairs={{64,0},{128,64},{192,128},{256,192},{320,256},{384,320},{448,384},... | collective-permute-start | bytes 73736 | tf_op jit(solution)/shard_map/ppermute | solution.py:42
  (8 other events, 58.8 us)
where the time goes:
time: 269 us; the launch traced here: 264 us
  blocking collectives  168 us (62%)
  starting transfers between devices  63.3 us (24%)
  waiting for transfers between devices  11.8 us (4%)
  between operations  11.2 us (4%)
  other arithmetic  6.8 us (3%)
    psum x12, blocking collectives, over_axes(): return functools.reduce(lax.psum, axes, value)  168 us
    ppermute x10, starting transfers between devices, padded_3(): lax.ppermute(last, axis, up)  28.4 us
    ppermute x10, starting transfers between devices, padded_3(): lax.ppermute(initial, axis, [(b, a) for a, b in up])  28 us
    ppermute x10, waiting for transfers between devices, padded_3(): lax.ppermute(initial, axis, [(b, a) for a, b in up])  10.5 us
  transfers between devices with their start and end apart: 24, of which 5 were waited for; matrix products, arithmetic and copies ran while one was open for 1% of the time, Pallas kernels for 0%

commit v1 on v0

v1 whole, which is shorter than its diff:
```python
import functools

import jax
import jax.numpy as jnp
from jax import lax
from jax.experimental import pallas as pl
from jax.experimental.pallas import tpu as pltpu
from jax.sharding import PartitionSpec as P

F32 = jnp.float32
NGX, NGY, CORES = 12, 64, 2
NX, NY, NZ = 8, 16, 128
HALO = 3
EX = NX + 2 * HALO
EY = 40
Y0 = 12
Y1 = Y0 + NY
B0, B1 = 8, 32
FACE_Z = 2.0
WELL_FACTOR = 4.0
N1 = NGX * CORES
N2 = NGY // CORES
TINY = 1e-30
SIDES = ((-1, 0), (1, 0), (0, -1), (0, 1))
CORNERS = ((-1, -1), (-1, 1), (1, -1), (1, 1))


def lookup(classes, table):
    values = [table[i] for i in range(16)]
    for bit in range(4):
        odd = (classes & (1 << bit)) != 0
        values = [
            jnp.where(odd, values[2 * j + 1], values[2 * j]) for j in range(len(values) // 2)
        ]
    return values[0]


def harmonic(a, b):
    return a * b / jnp.maximum(a + b, TINY)


def up(v):
    return pltpu.roll(v, NZ - 1, v.ndim - 1)


def down(v):
    return pltpu.roll(v, 1, v.ndim - 1)


def span(step, depth, start, length):
    if step == 0:
        return (start, length), (start, length)
    if step < 0:
        return (start, depth), (start + length, depth)
    return (start + length - depth, depth), (start - depth, depth)


def kernel(
    rock_h, well_h, perm_s, poro_s, accum_h, mobility_h, right_h,
    pressure_o, correction_o,
    rock, well, accum, right, mob,
    ext, v1, v2, cx, cy, cz, hx, hy, hz,
    poro_v, wterm, coef, binv, ys, zs,
    row1, row2, got1, got2,
    in_sem, main_send, main_recv, mob_send, mob_recv, ys_send, ys_recv, s1_send, s1_recv, s2_send, s2_recv,
):
    gx = lax.axis_index("gx")
    gy = lax.axis_index("gy")
    core = lax.rem(gy, CORES)
    plane = gy // CORES
    rank1 = gx * CORES + core

    def exists(step):
        ok = None
        for s, at, n in ((step[0], gx, NGX), (step[1], gy, NGY)):
            if s:
                this = at > 0 if s < 0 else at < n - 1
                ok = this if ok is None else jnp.logical_and(ok, this)
        return ok

    def on_sides(steps, action):
        for index, step in enumerate(steps):
            pl.when(exists(step))(functools.partial(action, index, step))

    def partner1(offset):
        other = lax.rem(rank1 + offset, N1)
        return (other // CORES, plane * CORES + lax.rem(other, CORES))

    def partner2(offset):
        return (gx, lax.rem(plane + offset, N2) * CORES + core)

    barrier = pltpu.get_barrier_semaphore()

    def greet(index, step):
        pl.semaphore_signal(barrier, inc=1, device_id=(gx + step[0], gy + step[1]))

    on_sides(SIDES + CORNERS, greet)

    @pl.loop(1, N1)
    def _(offset):
        pl.semaphore_signal(barrier, inc=1, device_id=partner1(offset))

    @pl.loop(1, N2)
    def _(offset):
        pl.semaphore_signal(barrier, inc=1, device_id=partner2(offset))

    loads = [
        pltpu.make_async_copy(s, d, in_sem.at[i])
        for i, (s, d) in enumerate(
            (
                (rock_h, rock),
                (well_h, well),
                (mobility_h, mob.at[:, 1 : NX + 1, Y0:Y1]),
                (right_h, right),
                (accum_h, accum),
            )
        )
    ]
    for copy in loads:
        copy.start()

    def closed(step):
        return jnp.logical_not(exists(step))

    for side, rows in ((-1, slice(0, HALO)), (1, slice(NX + HALO, EX))):

        @pl.when(closed((side, 0)))
        def _(side=side, rows=rows):
            ext[:, rows, B0:B1] = jnp.zeros((4, HALO, B1 - B0, NZ), F32)
            line = 0 if side < 0 else NX + 1
            ys[:, line, Y0:Y1] = jnp.zeros((12, NY, NZ), F32)
            mob[:, line, Y0:Y1] = jnp.zeros((3, NY, NZ), F32)

    for side, cols in ((-1, slice(8, Y0)), (1, slice(Y1, Y1 + 4))):

        @pl.when(closed((0, side)))
        def _(side=side, cols=cols):
            @pl.loop(0, EX)
            def _(i):
                ext[:, i, cols] = jnp.zeros((4, 4, NZ), F32)

            @pl.loop(0, NX + 2)
            def _(i):
                ys[:, i, cols] = jnp.zeros((12, 4, NZ), F32)
                mob[:, i, cols] = jnp.zeros((3, 4, NZ), F32)

    for copy in loads:
        copy.wait()

    @pl.loop(0, NX)
    def _(i):
        classes = rock[i]
        perm = lookup(classes, perm_s)
        poro = lookup(classes, poro_s)
        total = mob[0, i + 1, Y0:Y1] + mob[1, i + 1, Y0:Y1] + mob[2, i + 1, Y0:Y1]
        term = WELL_FACTOR * perm * well[i].astype(F32)
        stored = accum[0, 0, i]
        for p in range(3):
            for q in range(3):
                if p or q:
                    stored = stored + accum[p, q, i]
        poro_v[i] = poro
        wterm[i] = term
        ext[0, i + HALO, Y0:Y1] = right[0, i] + right[1, i] + right[2, i]
        ext[1, i + HALO, Y0:Y1] = perm
        ext[2, i + HALO, Y0:Y1] = total
        ext[3, i + HALO, Y0:Y1] = poro * stored + term * total

    pl.semaphore_wait(
        barrier,
        N1 - 1 + N2 - 1 + sum(exists(s).astype(jnp.int32) for s in SIDES + CORNERS),
    )

    def halo_copy(ref, steps, send, recv, depths, first_row, index, step, slot):
        (xs, xn), (xd, _) = span(step[0], depths[index], first_row, NX)
        (ysrc, yn), (yd, _) = span(step[1], depths[index], Y0, NY)
        return pltpu.make_async_remote_copy(
            ref.at[:, xs : xs + xn, ysrc : ysrc + yn],
            ref.at[:, xd : xd + xn, yd : yd + yn],
            send.at[index],
            recv.at[slot],
            device_id=(gx + step[0], gy + step[1]),
        )

    def exchange(ref, steps, send, recv, depths, first_row):
        make = functools.partial(halo_copy, ref, steps, send, recv, depths, first_row)

        def start(index, step):
            make(index, step, steps.index((-step[0], -step[1]))).start()

        def arrived(index, step):
            make(index, step, index).wait_recv()

        def sent(index, step):
            make(index, step, index).wait_send()

        return tuple(functools.partial(on_sides, steps, f) for f in (start, arrived, sent))

    steps8 = SIDES + CORNERS
    main_start, main_arrived, main_sent = exchange(
        ext, steps8, main_send, main_recv, (HALO,) * 4 + (2,) * 4, HALO
    )
    mob_start, mob_arrived, mob_sent = exchange(mob, SIDES, mob_send, mob_recv, (1,) * 4, 1)
    ys_start, ys_arrived, ys_sent = exchange(ys, SIDES, ys_send, ys_recv, (1,) * 4, 1)

    main_start()
    mob_start()
    main_arrived()

    low, mid, high = slice(B0 - 1, B1 - 1), slice(B0, B1), slice(B0 + 1, B1 + 1)
    lane = lax.broadcasted_iota(jnp.int32, (B1 - B0, NZ), 1)

    @pl.loop(0, EX - 1)
    def _(i):
        k = ext[1, i, mid]
        m = ext[2, i, mid]
        face = harmonic(k, ext[1, i + 1, mid])
        hx[i, mid] = face
        cx[i, mid] = face * (m + ext[2, i + 1, mid])
        face = harmonic(k, ext[1, i, high])
        hy[i, mid] = face
        cy[i, mid] = face * (m + ext[2, i, high])
        face = jnp.where(lane == NZ - 1, 0.0, FACE_Z * harmonic(k, up(k)))
        hz[i, mid] = face
        cz[i, mid] = face * (m + up(m))

    def operate(field, i, low, mid, high):
        own = field(i, mid)
        out = ext[3, i, mid] * own
        out = out + cx[i, mid] * (own - field(i + 1, mid))
        out = out + cx[i - 1, mid] * (own - field(i - 1, mid))
        out = out + cy[i, mid] * (own - field(i, high))
        out = out + cy[i, low] * (own - field(i, low))
        flux = cz[i, mid] * (own - up(own))
        return out + flux - down(flux), own

    of_v0 = lambda i, s: ext[0, i, s]
    of_v1 = lambda i, s: v1[i, s]
    of_v2 = lambda i, s: v2[i, s]

    @pl.loop(1, EX - 1)
    def _(i):
        v1[i, mid] = operate(of_v0, i, low, mid, high)[0]

    @pl.loop(2, EX - 2)
    def _(i):
        v2[i, mid] = operate(of_v1, i, low, mid, high)[0]

    own_y = slice(Y0, Y1)

    def moments(i, sums):
        image, second = operate(of_v2, i, slice(Y0 - 1, Y1 - 1), own_y, slice(Y0 + 1, Y1 + 1))
        zeroth, first = ext[0, i, own_y], v1[i, own_y]
        terms = (
            zeroth * zeroth, zeroth * first, first * first,
            first * second, second * second, second * image,
        )
        return tuple(s + t[:8] + t[8:] for s, t in zip(sums, terms))

    sums = lax.fori_loop(HALO, HALO + NX, moments, (jnp.zeros((8, NZ), F32),) * 6)
    sub = lax.broadcasted_iota(jnp.int32, (8, NZ), 0)
    lane8 = lax.broadcasted_iota(jnp.int32, (8, NZ), 1)
    stacked = jnp.zeros((8, NZ), F32)
    for n, s in enumerate(sums):
        stacked = jnp.where(sub == n, jnp.sum(s, axis=0, keepdims=True), stacked)
    per_row = jnp.sum(stacked, axis=1, keepdims=True)
    mine = jnp.sum(jnp.where(sub == lane8, per_row, 0.0), axis=0, keepdims=True)
    row1[0] = mine
    got1[rank1] = mine

    def copy1(offset):
        return pltpu.make_async_remote_copy(
            row1.at[0], got1.at[rank1], s1_send, s1_recv, device_id=partner1(offset)
        )

    def copy2(offset):
        return pltpu.make_async_remote_copy(
            row2.at[0], got2.at[plane], s2_send, s2_recv, device_id=partner2(offset)
        )

    @pl.loop(1, N1)
    def _(offset):
        copy1(offset).start()

    def whole1():
        part = got1.at[pl.ds(0, N1 - 1)]
        return pltpu.make_async_remote_copy(part, part, s1_send, s1_recv, device_id=partner1(1))

    def whole2():
        part = got2.at[pl.ds(0, N2 - 1)]
        return pltpu.make_async_remote_copy(part, part, s2_send, s2_recv, device_id=partner2(1))

    mob_arrived()
    fields = (of_v0, of_v1, of_v2)
    ylow, yhigh = slice(Y0 - 1, Y1 - 1), slice(Y0 + 1, Y1 + 1)

    @pl.loop(0, NX)
    def _(i):
        e, m = i + HALO, i + 1
        faces = (hx[e - 1, own_y], hx[e, own_y], hy[e, ylow], hy[e, own_y], hz[e, own_y])
        diagonal, couple = [], []
        for p in range(3):
            own = mob[p, m, own_y]
            c = [
                faces[0] * (mob[p, m - 1, own_y] + own),
                faces[1] * (mob[p, m + 1, own_y] + own),
                faces[2] * (mob[p, m, ylow] + own),
                faces[3] * (mob[p, m, yhigh] + own),
            ]
            vertical = faces[4] * (own + up(own))
            c += [down(vertical), vertical]
            for n in range(6):
                coef[p, n, i] = c[n]
            couple.append(c)
            diagonal.append(c[0] + c[1] + c[2] + c[3] + c[4] + c[5] + wterm[i] * own)
        poro = poro_v[i]
        b = [[poro * accum[p, q, i] for q in range(3)] for p in range(3)]
        for p in range(3):
            b[p][p] = b[p][p] + diagonal[p]
        adj = [[None] * 3 for _ in range(3)]
        for p in range(3):
            for q in range(3):
                r1, r2, c1, c2 = (q + 1) % 3, (q + 2) % 3, (p + 1) % 3, (p + 2) % 3
                adj[p][q] = b[r1][c1] * b[r2][c2] - b[r1][c2] * b[r2][c1]
        inverse = 1.0 / (b[0][0] * adj[0][0] + b[0][1] * adj[1][0] + b[0][2] * adj[2][0])
        inv = [[adj[p][q] * inverse for q in range(3)] for p in range(3)]
        for p in range(3):
            for q in range(3):
                binv[3 * p + q, i] = inv[p][q]

        def solve(side):
            return [inv[p][0] * side[0] + inv[p][1] * side[1] + inv[p][2] * side[2] for p in range(3)]

        first = solve([right[p, i] for p in range(3)])
        for p in range(3):
            ys[p, m, own_y] = first[p]
        for n, field in enumerate(fields):
            own = field(e, own_y)
            near = (
                field(e - 1, own_y), field(e + 1, own_y), field(e, ylow), field(e, yhigh),
                down(own), up(own),
            )
            side = []
            for p in range(3):
                t = couple[p][0] * near[0]
                for d in range(1, 6):
                    t = t + couple[p][d] * near[d]
                side.append(t)
            result = solve(side)
            for p in range(3):
                ys[3 * n + 3 + p, m, own_y] = result[p]

    ys_start()

    whole1().wait_recv()
    total = got1[0]
    for n in range(1, N1):
        total = total + got1[n]
    row2[0] = total
    got2[plane] = total

    @pl.loop(1, N2)
    def _(offset):
        copy2(offset).start()

    ys_arrived()

    @pl.loop(0, NX)
    def _(i):
        m = i + 1
        for n in range(4):
            side = []
            for p in range(3):
                f = 3 * n + p
                own = ys[f, m, own_y]
                near = (
                    ys[f, m - 1, own_y], ys[f, m + 1, own_y], ys[f, m, ylow], ys[f, m, yhigh],
                    down(own), up(own),
                )
                t = coef[p, 0, i] * near[0]
                for d in range(1, 6):
                    t = t + coef[p, d, i] * near[d]
                side.append(t + right[p, i] if n == 0 else t)
            for p in range(3):
                zs[3 * n + p, i] = (
                    binv[3 * p, i] * side[0] + binv[3 * p + 1, i] * side[1] + binv[3 * p + 2, i] * side[2]
                )

    whole2().wait_recv()
    total = got2[0]
    for n in range(1, N2):
        total = total + got2[n]
    nu = [jnp.broadcast_to(total[:, n : n + 1], (1, NZ)) for n in range(6)]

    def guarded(pivot, scale):
        good = pivot > 1e-7 * scale
        return jnp.where(good, 1.0 / jnp.where(good, pivot, 1.0), 0.0)

    r0 = guarded(nu[1], 0.0)
    l10 = nu[2] * r0
    l20 = nu[3] * r0
    d1 = nu[3] - l10 * nu[2]
    t21 = nu[4] - l20 * nu[2]
    r1 = guarded(d1, nu[3])
    l21 = t21 * r1
    d2 = nu[5] - l20 * nu[3] - l21 * t21
    r2 = guarded(d2, nu[5])
    y1 = nu[1] - l10 * nu[0]
    y2 = nu[2] - l20 * nu[0] - l21 * y1
    a2 = y2 * r2
    a1 = y1 * r1 - l21 * a2
    a0 = nu[0] * r0 - l10 * a1 - l20 * a2
    a0, a1, a2 = (jnp.broadcast_to(a, (NY, NZ)) for a in (a0, a1, a2))

    @pl.loop(0, NX)
    def _(i):
        e = i + HALO
        pressure_o[i] = a0 * ext[0, e, own_y] + a1 * v1[e, own_y] + a2 * v2[e, own_y]
        for p in range(3):
            correction_o[p, i] = zs[p, i] + a0 * zs[3 + p, i] + a1 * zs[6 + p, i] + a2 * zs[9 + p, i]

    main_sent()
    mob_sent()
    ys_sent()
    whole1().wait_send()
    whole2().wait_send()


def shards(rock_class, well_mask, perm_table, poro_table, accum, mobility, right_side):
    any_spec = pl.BlockSpec(memory_space=pl.ANY)
    smem = pl.BlockSpec(memory_space=pltpu.SMEM)
    vmem = pl.BlockSpec(memory_space=pltpu.VMEM)
    field = (NX, NY, NZ)
    dma = pltpu.SemaphoreType.DMA
    return tuple(
        pl.pallas_call(
            kernel,
            name="cpr",
            out_shape=(
                jax.ShapeDtypeStruct(field, F32),
                jax.ShapeDtypeStruct((3,) + field, F32),
            ),
            in_specs=[any_spec, any_spec, smem, smem, any_spec, any_spec, any_spec],
            out_specs=(vmem, vmem),
            scratch_shapes=[
                pltpu.VMEM(field, jnp.int32),
                pltpu.VMEM(field, jnp.int32),
                pltpu.VMEM((3, 3) + field, F32),
                pltpu.VMEM((3,) + field, F32),
                pltpu.VMEM((3, NX + 2, EY, NZ), F32),
                pltpu.VMEM((4, EX, EY, NZ), F32),
            ]
            + [pltpu.VMEM((EX, EY, NZ), F32)] * 8
            + [
                pltpu.VMEM(field, F32),
                pltpu.VMEM(field, F32),
                pltpu.VMEM((3, 6) + field, F32),
                pltpu.VMEM((9,) + field, F32),
                pltpu.VMEM((12, NX + 2, EY, NZ), F32),
                pltpu.VMEM((12,) + field, F32),
                pltpu.VMEM((1, 1, NZ), F32),
                pltpu.VMEM((1, 1, NZ), F32),
                pltpu.VMEM((N1, 1, NZ), F32),
                pltpu.VMEM((N2, 1, NZ), F32),
                dma((5,)),
                dma((8,)), dma((8,)), dma((4,)), dma((4,)), dma((4,)), dma((4,)),
                dma, dma, dma, dma,
            ],
            compiler_params=pltpu.CompilerParams(collective_id=0, has_side_effects=True),
        )(rock_class, well_mask, perm_table, poro_table, accum, mobility, right_side)
    )


def solution(mesh):
    in_specs = (
        P("gx", "gy", None),
        P("gx", "gy", None),
        P(),
        P(),
        P(None, None, "gx", "gy", None),
        P(None, "gx", "gy", None),
        P(None, "gx", "gy", None),
    )
    out_specs = (P("gx", "gy", None), P(None, "gx", "gy", None))
    return jax.shard_map(shards, mesh=mesh, in_specs=in_specs, out_specs=out_specs, check_vma=False)
```

time: 269 us -> 48.2 us (0.18); the launches traced: 264 us -> 48 us
  blocking collectives: 168 us -> 0 us
  starting transfers between devices: 63.3 us -> 0 us
  Pallas kernels: 0 us -> 44.2 us
  waiting for transfers between devices: 11.8 us -> 0 us
  between operations: 11.2 us -> 0.64 us
  other arithmetic: 6.8 us -> 0 us
    psum x12 -> x0, blocking collectives: 168 us -> none  [over_axes(): return functools.reduce(lax.psum, axes, value)]
    ppermute x24 -> x0, starting transfers between devices: 63.3 us -> none  [the longest x10 28.4 us: padded_3(): lax.ppermute(last, axis, up)]
    pallas_call x0 -> x1, Pallas kernels: none -> 44.2 us  [shards(): pl.pallas_call(kernel, name='cpr', out_shape=(jax.ShapeDtypeStruct(field,...]
    ppermute x24 -> x0, waiting for transfers between devices: 11.8 us -> none  [the longest x10 10.5 us: padded_3(): lax.ppermute(initial, axis, [(b, a) for a, b in up])]
    reduce_sum x13 -> x0, other arithmetic: 4.32 us -> none  [the longest x3 2.16 us: shards(): jnp.sum(applied * residual)]
  transfers between devices with their start and end apart: 24 -> 0, of which waited for: 5 -> 0; matrix products, arithmetic and copies ran while one was open for 1% -> 0% of each run, Pallas kernels for 0% -> 0%
where the time goes in v1:
time: 48.2 us; the launch traced here: 48 us
  Pallas kernels  44.2 us (92%)
  local copies, waits for them, and re-layouts  3.09 us (6%)
  between operations  0.64 us (1%)
    pallas_call x1, Pallas kernels, shards(): pl.pallas_call(kernel, name='cpr', out_shape=(jax.ShapeDtypeStruct(field,...  44.2 us
    unnamed x2, local copies, waits for them, and re-layouts  3.09 us

profile of v1, /device:TPU:1, one launch (start us, length us, event | category | flops | bytes accessed | tf_op | source)
XLA Modules:
  0.0 48.0 jit_solution(860659843202195593)
XLA Ops:
  0.6 44.2 %cpr.1 = (f32[8,16,128]{2,1,0:T(8,128)}, f32[3,8,16,128]{3,2,1,0:T(8,128)}) custom-call(s32[8,16,128]{2,1,0:T(8,128)} %rock_h.1, s32[8,16,128]{2,1,0:T(8,128)} %well_h.1, f32[16]{0:T(128)} %perm_s.1, f32[16]{0:T(128)} %poro_s.1, f32[3,3,8,16,128]{4,3,2,1,0:T(8,128)} %accum_h.1, f32[3,8,16,128]{3,2,1,0:T(8,128)} %mobility_h.1, f32[3,8,16,128]{3,2,1,0:T(8,128)} %right_h.1), custom_call_target="tpu_custom_call" | custom-call | tf_op jit(solution)/shard_map/cpr/pallas_call | solution.py:436
  44.9 1.5 %copy.11 = f32[8,16,128]{2,1,0:T(8,128)} copy(f32[8,16,128]{2,1,0:T(8,128)} %get-tuple-element.4) | data formatting | bytes 131072
  46.3 1.6 %copy.12 = f32[3,8,16,128]{3,2,1,0:T(8,128)} copy(f32[3,8,16,128]{3,2,1,0:T(8,128)} %get-tuple-element.5) | data formatting | bytes 393216
